TPU v7x, 512 devices: a whole 4x8x8 slice. The times are simulated.
512 devices in a mesh: dp: 32 (over x, y), tensor: 16 (over z, core).
Axes of the slice: x: 4, y: 8, z: 8, core: 2. Of those that a mesh axis runs over, the one named last changes fastest.
Arguments:
- queries: bfloat16 [4096, 16384], P('dp', 'tensor'), may hold values from -24 to 24
- draft_keys: bfloat16 [4096, 1024], P('dp'), may hold values from -6 to 6
- draft_values: bfloat16 [4096, 1024], P('dp'), may hold values from -6 to 6
- cache_keys: bfloat16 [64, 2048, 1024], P('dp', 'tensor'), may hold values from -24 to 24
- cache_values: bfloat16 [64, 2048, 1024], P('dp', 'tensor'), may hold values from -6 to 6
- out_weight: bfloat16 [16384, 16384], P('tensor', 'dp'), may hold values from -0.25 to 0.25
- cache_lengths: int32 [64], P('dp'), may hold values from 512 to 2048
- draft_lengths: int32 [64], replicated, may hold values from 8 to 64
- dest_group: int32 [64], replicated, may hold values from 0 to 31, as said below
- dest_offset: int32 [64], replicated, may hold values from 0 to 32, as said below
Outputs:
- verified: bfloat16 [3072, 16384], P('tensor', 'dp')
Inputs may be any that keep to these rules, and one draw needn't show every extreme that they name: `dest_group`: at most one request of a group has another group as destination, and each group receives at most one such request. `dest_offset`: blocks with the same destination never intersect and end at packed row 96 or before; a block moved to another group starts right after that group's own rows; in every draw some group's blocks fill all 96 rows.
All inputs are finite; a program needn't handle non-finite values.
Results may differ from a plain program's by a relative error of at most 0.017.
Values may be sent and summed in bfloat16 or wider, within the bound.
No kernel may reach another device: no remote copies, remote signals or barrier semaphores. Data moves between devices by JAX's collectives and lax.ppermute only.
A program may use at most 64 MiB of HBM per device.

v0:
```python
import jax
import jax.numpy as jnp
from jax import lax
from jax.sharding import PartitionSpec as P

HEADS = 128
KV_HEADS = 8
HEAD_DIM = 128
DRAFT = 64
GROUP_REQ = 2
PACK = 96
NEG_FILL = -1e30


def packed_sources(row_ids, draft_lengths, dest_group, dest_offset):
    request_ids = jnp.arange(dest_group.shape[0], dtype=jnp.int32)
    slot_group = row_ids // PACK
    slot_index = row_ids % PACK
    inside = (
        (dest_group[None, :] == slot_group[:, None])
        & (slot_index[:, None] >= dest_offset[None, :])
        & (slot_index[:, None] < (dest_offset + draft_lengths)[None, :])
    )
    request = jnp.sum(jnp.where(inside, request_ids[None, :], 0), axis=1)
    first_slot = jnp.sum(jnp.where(inside, dest_offset[None, :], 0), axis=1)
    return (request, slot_index - first_slot, jnp.any(inside, axis=1))


def attend_one(operands):
    queries_one, cache_k, cache_v, draft_k, draft_v, cache_len, draft_len = operands
    score_scale = HEAD_DIM ** (-0.5)
    cache_scores = (
        jnp.einsum("qkgd,lkd->kgql", queries_one, cache_k, preferred_element_type=jnp.float32)
        * score_scale
    )
    draft_scores = (
        jnp.einsum("qkgd,jkd->kgqj", queries_one, draft_k, preferred_element_type=jnp.float32)
        * score_scale
    )
    cache_pos = jnp.arange(cache_k.shape[0], dtype=jnp.int32)
    draft_pos = jnp.arange(draft_k.shape[0], dtype=jnp.int32)
    keep_cache = cache_pos < cache_len
    keep_draft = (draft_pos[None, :] <= draft_pos[:, None]) & (draft_pos[None, :] < draft_len)
    cache_scores = jnp.where(keep_cache, cache_scores, NEG_FILL)
    draft_scores = jnp.where(keep_draft, draft_scores, NEG_FILL)
    highest = jnp.maximum(
        jnp.max(cache_scores, axis=-1, keepdims=True), jnp.max(draft_scores, axis=-1, keepdims=True)
    )
    cache_exp = jnp.exp(cache_scores - highest)
    draft_exp = jnp.exp(draft_scores - highest)
    denominator = jnp.sum(cache_exp, axis=-1, keepdims=True) + jnp.sum(
        draft_exp, axis=-1, keepdims=True
    )
    cache_weights = (cache_exp / denominator).astype(jnp.bfloat16)
    draft_weights = (draft_exp / denominator).astype(jnp.bfloat16)
    mixed = jnp.einsum("kgql,lkd->qkgd", cache_weights, cache_v, preferred_element_type=jnp.float32)
    mixed = mixed + jnp.einsum(
        "kgqj,jkd->qkgd", draft_weights, draft_v, preferred_element_type=jnp.float32
    )
    is_live = draft_pos < draft_len
    return jnp.where(is_live[:, None, None, None], mixed, 0.0).astype(jnp.bfloat16)


def body(
    queries,
    draft_keys,
    draft_values,
    cache_keys,
    cache_values,
    out_weight,
    cache_lengths,
    draft_lengths,
    dest_group,
    dest_offset,
):
    tensor_count = lax.axis_size("tensor")
    data_count = lax.axis_size("dp")
    my_rank = lax.axis_index("tensor")
    my_group = lax.axis_index("dp")
    local_heads = HEADS // tensor_count
    group_heads = HEADS // KV_HEADS
    kv_local = max(1, local_heads // group_heads)
    per_kv = local_heads // kv_local
    kv_width = kv_local * HEAD_DIM
    span_rows = cache_keys.shape[1]
    copies = tensor_count // KV_HEADS

    def spread(cache_block):
        return jnp.repeat(
            cache_block.reshape(GROUP_REQ, span_rows, KV_HEADS, HEAD_DIM), copies, axis=2
        )

    full_keys, full_values = (
        lax.all_to_all(spread(cache_keys), "tensor", split_axis=2, concat_axis=1, tiled=True),
        lax.all_to_all(spread(cache_values), "tensor", split_axis=2, concat_axis=1, tiled=True),
    )
    kv_first = my_rank * local_heads // group_heads
    draft_k = lax.dynamic_slice_in_dim(draft_keys, kv_first * HEAD_DIM, kv_width, 1).reshape(
        GROUP_REQ, DRAFT, kv_local, HEAD_DIM
    )
    draft_v = lax.dynamic_slice_in_dim(draft_values, kv_first * HEAD_DIM, kv_width, 1).reshape(
        GROUP_REQ, DRAFT, kv_local, HEAD_DIM
    )
    local_queries = queries.reshape(GROUP_REQ, DRAFT, kv_local, per_kv, HEAD_DIM)
    my_lengths = lax.dynamic_slice_in_dim(draft_lengths, my_group * GROUP_REQ, GROUP_REQ)
    attended = lax.map(
        attend_one,
        (local_queries, full_keys, full_values, draft_k, draft_v, cache_lengths, my_lengths),
    )
    width_local = local_heads * HEAD_DIM
    attended_rows = attended.reshape(GROUP_REQ * DRAFT, width_local)
    target_rows = PACK * data_count // tensor_count
    home_all = lax.all_gather(attended_rows, "dp", axis=0, tiled=True)
    row_ids = jnp.arange(lax.axis_size("tensor") * target_rows, dtype=jnp.int32)
    request, within, is_live = packed_sources(row_ids, draft_lengths, dest_group, dest_offset)
    picked = jnp.take(home_all, request * DRAFT + within, axis=0)
    picked = jnp.where(is_live[:, None], picked, jnp.zeros((), jnp.bfloat16))
    return lax.psum_scatter(
        jnp.dot(picked, out_weight, preferred_element_type=jnp.float32).astype(jnp.bfloat16),
        "tensor",
        scatter_dimension=0,
        tiled=True,
    )


def solution(mesh):
    in_specs = (
        P("dp", "tensor"),
        P("dp", None),
        P("dp", None),
        P("dp", "tensor", None),
        P("dp", "tensor", None),
        P("tensor", "dp"),
        P("dp"),
        P(),
        P(),
        P(),
    )
    out_specs = P("tensor", "dp")
    return jax.shard_map(body, mesh=mesh, in_specs=in_specs, out_specs=out_specs, check_vma=False)
```

profile of v0, /device:TPU:8, one launch (start us, length us, event | category | flops | bytes accessed | tf_op | source)
XLA Modules:
  0.0 296.0 jit_solution(7023909836648568548)
XLA Ops:
  6.5 1.3 copy_bitcast_fusion.3
  7.9 1.2 broadcast_in_dim.102
  9.1 10.4 %all-to-all-start.1 = ((bf16[2,128,16,128]{3,1,0,2:T(8,128)(2,1)}), bf16[2,128,16,128]{3,1,0,2:T(8,128)(2,1)S(1)}, u32[]{:S(2)}, u32[]{:S(2)}) async-start(bf16[2,128,16,128]{3,1,0,2:T(8,128)(2,1)} %bitcast.25), calls=%async_computation.1 | async-start | bytes 2097152 | tf_op jit(solution)/shard_map/all_to_all | solution.py:94
  19.7 26.3 %all-to-all-done.1 = bf16[2,128,16,128]{3,1,0,2:T(8,128)(2,1)S(1)} async-done(((bf16[2,128,16,128]{3,1,0,2:T(8,128)(2,1)}), bf16[2,128,16,128]{3,1,0,2:T(8,128)(2,1)S(1)}, u32[]{:S(2)}, u32[]{:S(2)}) %all-to-all-start.1) | async-done | bytes 1048608 | tf_op jit(solution)/shard_map/all_to_all | solution.py:94
  46.0 1.3 broadcast_in_dim.101
  47.3 5.0 %all-to-all-start = ((bf16[2,128,16,128]{3,1,0,2:T(8,128)(2,1)}), bf16[2,128,16,128]{3,1,0,2:T(8,128)(2,1)}, u32[]{:S(2)}, u32[]{:S(2)}) async-start(bf16[2,128,16,128]{3,1,0,2:T(8,128)(2,1)} %bitcast.20), calls=%async_computation | async-start | bytes 2097152 | tf_op jit(solution)/shard_map/all_to_all | solution.py:95
  52.5 0.8 constant_dynamic-slice_fusion.1
  53.4 25.4 %all-to-all-done = bf16[2,128,16,128]{3,1,0,2:T(8,128)(2,1)} async-done(((bf16[2,128,16,128]{3,1,0,2:T(8,128)(2,1)}), bf16[2,128,16,128]{3,1,0,2:T(8,128)(2,1)}, u32[]{:S(2)}, u32[]{:S(2)}) %all-to-all-start) | async-done | bytes 1048608 | tf_op jit(solution)/shard_map/all_to_all | solution.py:95
  78.8 1.3 copy.36
  80.1 14.2 %while.10 = (s32[]{:T(128)}, bf16[2,64,1,8,128]{4,3,1,0,2:T(8,128)(2,1)}, s32[2]{0:T(128)S(1)}, bf16[2,2048,1,128]{3,1,2,0:T(8,128)(2,1)S(1)}, s32[2]{0:T(128)S(...) while((s32[]{:T(128)}, ...), condition=%wide.region_8.9_spmd, body=%wide.region_3.8_spmd.sunk | while | flops 566699072 | bytes 15692581 | solution.py:106
  83.2 0.9 bitcast_reduce_fusion.2
  84.2 0.9 fusion.71
  85.1 1.1 fusion.73
  86.5 0.7 copy_dynamic-update-slice_fusion.2
  89.3 0.7 iota_compare_fusion.5
  90.3 0.9 bitcast_reduce_fusion.2
  91.3 0.9 fusion.71
  92.2 1.1 fusion.73
  93.6 0.7 copy_dynamic-update-slice_fusion.2
  94.3 1.7 copy.62
  97.0 99.9 %all-gather.2.cloned.1.call-done = bf16[4096,1024]{1,0:T(8,128)(2,1)} async-done(((bf16[128,1024]{1,0:T(8,128)(2,1)}), bf16[4096,1024]{1,0:T(8,128)(2,1)}) %all-gather.2.cloned.1.call-update) | async-done | bytes 8388624 | tf_op jit(solution)/shard_map/all_gather | solution.py:113
  196.9 20.4 %gather_fusion = bf16[3072,1024]{1,0:T(8,128)(2,1)} fusion(bf16[4096,1024]{1,0:T(8,128)(2,1)} %all-gather.2.cloned.1.call-done, s32[3072]{0:T(1024)S(1)} %broadcast_clamp_fusion), kind=kCustom, calls=%fused_computation | custom fusion | bytes 12595200 | tf_op jit(solution)/shard_map/jit(_take)/gather | solution.py:116
  217.3 7.6 %fusion.34 = bf16[3072,512]{1,0:T(8,128)(2,1)} fusion(bf16[1024,512]{1,0:T(8,128)(2,1)S(1)} %copy-done, bf16[3072,1024]{1,0:T(8,128)(2,1)} %gather_fusion, pred[3072]{0:T(1024)(128)(4,1)S(1)} %compare_and_fusion.1, pred[3072]{0:T(1024)(128)(4,1)S(1)} %fusion.50), kind=kOutput, calls=%fused_computation.49 | convolution fusion | flops 3229089792 | bytes 10491904 | tf_op jit(solution)/shard_map/dot_general | solution.py:119
  224.9 64.2 %reduce-scatter.2.cloned.1.call-done = bf16[192,512]{1,0:T(8,128)(2,1)} async-done(((bf16[3072,512]{1,0:T(8,128)(2,1)}), bf16[192,512]{1,0:T(8,128)(2,1)}) %reduce-scatter.2.cloned.1.call-update) | async-done | bytes 196624 | tf_op jit(solution)/shard_map/reduce_scatter | solution.py:118
  (52 shorter events, 7.4 us)
Async XLA Ops:
  6.5 210.7 %copy-start = (bf16[1024,512]{1,0:T(8,128)(2,1)S(1)}, bf16[1024,512]{1,0:T(8,128)(2,1)}, u32[]{:S(2)}) copy-start(bf16[1024,512]{1,0:T(8,128)(2,1)} %param.17) | copy-start | bytes 3145732
  6.5 13.0 %copy-start.1 = (bf16[2,128,1024]{2,1,0:T(8,128)(2,1)S(1)}, bf16[2,128,1024]{2,1,0:T(8,128)(2,1)}, u32[]{:S(2)}) copy-start(bf16[2,128,1024]{2,1,0:T(8,128)(2,1)} %param.16) | copy-start | bytes 1572868
  7.8 44.5 %copy-start.2 = (bf16[128,1024]{1,0:T(8,128)(2,1)S(1)}, bf16[128,1024]{1,0:T(8,128)(2,1)}, u32[]{:S(2)}) copy-start(bf16[128,1024]{1,0:T(8,128)(2,1)} %param.12) | copy-start | bytes 786436
  7.8 44.6 %copy-start.6 = (s32[64]{0:T(128)S(1)}, s32[64]{0:T(128)}, u32[]{:S(2)}) copy-start(s32[64]{0:T(128)} %param.19) | copy-start | bytes 772
  9.1 36.9 %all-to-all-start.1 = ((bf16[2,128,16,128]{3,1,0,2:T(8,128)(2,1)}), bf16[2,128,16,128]{3,1,0,2:T(8,128)(2,1)S(1)}, u32[]{:S(2)}, u32[]{:S(2)}) async-start(bf16[2,128,16,128]{3,1,0,2:T(8,128)(2,1)} %bitcast.25), calls=%async_computation.1 | async-start | bytes 2097152 | tf_op jit(solution)/shard_map/all_to_all | solution.py:94
  19.7 60.4 %copy-start.5 = (s32[2]{0:T(128)S(1)}, s32[2]{0:T(128)}, u32[]{:S(2)}) copy-start(s32[2]{0:T(128)} %param.18) | copy-start | bytes 28
  47.3 31.5 %all-to-all-start = ((bf16[2,128,16,128]{3,1,0,2:T(8,128)(2,1)}), bf16[2,128,16,128]{3,1,0,2:T(8,128)(2,1)}, u32[]{:S(2)}, u32[]{:S(2)}) async-start(bf16[2,128,16,128]{3,1,0,2:T(8,128)(2,1)} %bitcast.20), calls=%async_computation | async-start | bytes 2097152 | tf_op jit(solution)/shard_map/all_to_all | solution.py:95
  52.3 144.6 %all-gather.2.cloned.1.call-start = ((), (), s32[]{:S(2)}) async-start(), calls=%async_computation.3 | async-start | bytes 8650752 | tf_op jit(solution)/shard_map/all_gather | solution.py:113
  80.1 16.0 %copy-start.3 = (s32[64]{0:T(128)S(1)}, s32[64]{0:T(128)}, u32[]{:S(2)}) copy-start(s32[64]{0:T(128)} %param.21) | copy-start | bytes 772
  80.1 16.0 %copy-start.4 = (s32[64]{0:T(128)S(1)}, s32[64]{0:T(128)}, u32[]{:S(2)}) copy-start(s32[64]{0:T(128)} %param.20) | copy-start | bytes 772
  96.0 193.2 %reduce-scatter.2.cloned.1.call-start = ((), (), s32[]{:S(2)}) async-start(), calls=%async_computation.4 | async-start | bytes 3342336 | tf_op jit(solution)/shard_map/reduce_scatter | solution.py:118
Sparse Core Ops, SparseCore 0:
  96.1 100.6 all-gather.1
  225.1 64.0 reduce-scatter.1
where the time goes:
time: 297 us; the launch traced here: 296 us
  waiting for transfers between devices  216 us (73%)
  local copies, waits for them, and re-layouts  32.5 us (11%)
  starting transfers between devices  15.5 us (5%)
  between operations  13.6 us (5%)
  matrix products  12.5 us (4%)
  other arithmetic  5.82 us (2%)
    all_gather x1, waiting for transfers between devices, body(): home_all = lax.all_gather(attended_rows, 'dp', axis=0, tiled=True)  99.9 us
    reduce_scatter x1, waiting for transfers between devices, body(): lax.psum_scatter(jnp.dot(picked, out_weight, preferred_element_type=jnp.f...  64.2 us
    all_to_all x1, waiting for transfers between devices, body(): lax.all_to_all(spread(cache_keys), 'tensor', split_axis=2, concat_axis=1,...  26.3 us
    all_to_all x1, waiting for transfers between devices, body(): lax.all_to_all(spread(cache_values), 'tensor', split_axis=2, concat_axis=...  25.4 us
    gather x1, local copies, waits for them, and re-layouts, body(): picked = jnp.take(home_all, request * DRAFT + within, axis=0)  20.4 us
    all_to_all x1, starting transfers between devices, body(): lax.all_to_all(spread(cache_keys), 'tensor', split_axis=2, concat_axis=1,...  10.4 us
    dot_general x1, matrix products, body(): jnp.dot(picked, out_weight, preferred_element_type=jnp.float32)  7.65 us
  transfers between devices with their start and end apart: 4, of which 4 were waited for; matrix products, arithmetic and copies ran while one was open for 1% of the time, Pallas kernels for 0%

commit v1 on v0

--- a/solution.py
+++ b/solution.py
@@ -110,7 +110,11 @@
     width_local = local_heads * HEAD_DIM
     attended_rows = attended.reshape(GROUP_REQ * DRAFT, width_local)
     target_rows = PACK * data_count // tensor_count
-    home_all = lax.all_gather(attended_rows, "dp", axis=0, tiled=True)
+    size = lax.axis_size("dp")
+    repeats = [size if d == 0 else 1 for d in range(attended_rows.ndim)]
+    home_all = lax.all_to_all(
+        jnp.tile(attended_rows, repeats), "dp", split_axis=0, concat_axis=0, tiled=True
+    )
     row_ids = jnp.arange(lax.axis_size("tensor") * target_rows, dtype=jnp.int32)
     request, within, is_live = packed_sources(row_ids, draft_lengths, dest_group, dest_offset)
     picked = jnp.take(home_all, request * DRAFT + within, axis=0)

time: 297 us -> 408 us (1.37)
  waiting for transfers between devices: 216 us -> 312 us
  starting transfers between devices: 15.5 us -> 25.7 us
  local copies, waits for them, and re-layouts: 32.5 us -> 36.8 us
    all_to_all x0 -> x1, waiting for transfers between devices: none -> 194 us  [body(): lax.all_to_all(jnp.tile(attended_rows, repeats), 'dp', split_axis=0, conc...]
    all_gather x1 -> x0, waiting for transfers between devices: 99.9 us -> none  [body(): home_all = lax.all_gather(attended_rows, 'dp', axis=0, tiled=True)]
    all_to_all x0 -> x1, starting transfers between devices: none -> 10.3 us  [body(): lax.all_to_all(jnp.tile(attended_rows, repeats), 'dp', split_axis=0, conc...]
    all_to_all x1, starting transfers between devices: 10.4 us -> 4.93 us  [body(): lax.all_to_all(spread(cache_keys), 'tensor', split_axis=2, concat_axis=1,...]
    all_to_all x1, starting transfers between devices: 4.98 us -> 10.4 us  [body(): lax.all_to_all(spread(cache_values), 'tensor', split_axis=2, concat_axis=...]
    another operation x0 -> x1, local copies, waits for them, and re-layouts: none -> 4.28 us  [body(): jnp.tile(attended_rows, repeats)]
    reduce_scatter x1, waiting for transfers between devices: 64.2 us -> 68.4 us  [body(): lax.psum_scatter(jnp.dot(picked, out_weight, preferred_element_type=jnp.f...]
where the time goes in v1:
time: 408 us; the launch traced here: 407 us
  waiting for transfers between devices  312 us (76%)
  local copies, waits for them, and re-layouts  36.8 us (9%)
  starting transfers between devices  25.7 us (6%)
  between operations  13.6 us (3%)
  matrix products  12.5 us (3%)
  other arithmetic  5.83 us (1%)
    all_to_all x1, waiting for transfers between devices, body(): lax.all_to_all(jnp.tile(attended_rows, repeats), 'dp', split_axis=0, conc...  194 us
    reduce_scatter x1, waiting for transfers between devices, body(): lax.psum_scatter(jnp.dot(picked, out_weight, preferred_element_type=jnp.f...  68.4 us
    all_to_all x1, waiting for transfers between devices, body(): lax.all_to_all(spread(cache_values), 'tensor', split_axis=2, concat_axis=...  26.3 us
    all_to_all x1, waiting for transfers between devices, body(): lax.all_to_all(spread(cache_keys), 'tensor', split_axis=2, concat_axis=1,...  23.5 us
    gather x1, local copies, waits for them, and re-layouts, body(): picked = jnp.take(home_all, request * DRAFT + within, axis=0)  20.4 us
    all_to_all x1, starting transfers between devices, body(): lax.all_to_all(spread(cache_values), 'tensor', split_axis=2, concat_axis=...  10.4 us
    all_to_all x1, starting transfers between devices, body(): lax.all_to_all(jnp.tile(attended_rows, repeats), 'dp', split_axis=0, conc...  10.3 us
  transfers between devices with their start and end apart: 4, of which 4 were waited for; matrix products, arithmetic and copies ran while one was open for 1% of the time, Pallas kernels for 0%

profile of v1, /device:TPU:8, one launch (start us, length us, event | category | flops | bytes accessed | tf_op | source)
XLA Modules:
  0.0 407.1 jit_solution(17798751463874585295)
XLA Ops:
  6.5 1.3 copy_bitcast_fusion.4
  7.8 1.2 broadcast_in_dim.101
  9.1 10.4 %all-to-all-start = ((bf16[2,128,16,128]{3,1,0,2:T(8,128)(2,1)}), bf16[2,128,16,128]{3,1,0,2:T(8,128)(2,1)S(1)}, u32[]{:S(2)}, u32[]{:S(2)}) async-start(bf16[2,128,16,128]{3,1,0,2:T(8,128)(2,1)} %bitcast.20), calls=%async_computation | async-start | bytes 2097152 | tf_op jit(solution)/shard_map/all_to_all | solution.py:95
  19.7 26.3 %all-to-all-done = bf16[2,128,16,128]{3,1,0,2:T(8,128)(2,1)S(1)} async-done(((bf16[2,128,16,128]{3,1,0,2:T(8,128)(2,1)}), bf16[2,128,16,128]{3,1,0,2:T(8,128)(2,1)S(1)}, u32[]{:S(2)}, u32[]{:S(2)}) %all-to-all-start) | async-done | bytes 1048608 | tf_op jit(solution)/shard_map/all_to_all | solution.py:95
  46.0 1.3 broadcast_in_dim.102
  47.3 4.9 %all-to-all-start.1 = ((bf16[2,128,16,128]{3,1,0,2:T(8,128)(2,1)}), bf16[2,128,16,128]{3,1,0,2:T(8,128)(2,1)S(1)}, u32[]{:S(2)}, u32[]{:S(2)}) async-start(bf16[2,128,16,128]{3,1,0,2:T(8,128)(2,1)} %bitcast.163), calls=%async_computation.1 | async-start | bytes 2097152 | tf_op jit(solution)/shard_map/all_to_all | solution.py:94
  52.2 1.0 copy.48
  53.3 0.8 constant_dynamic-slice_fusion.1
  54.1 1.1 copy.35
  55.2 23.5 %all-to-all-done.1 = bf16[2,128,16,128]{3,1,0,2:T(8,128)(2,1)S(1)} async-done(((bf16[2,128,16,128]{3,1,0,2:T(8,128)(2,1)}), bf16[2,128,16,128]{3,1,0,2:T(8,128)(2,1)S(1)}, u32[]{:S(2)}, u32[]{:S(2)}) %all-to-all-start.1) | async-done | bytes 1048608 | tf_op jit(solution)/shard_map/all_to_all | solution.py:94
  78.8 14.2 %while.10 = (s32[]{:T(128)}, bf16[2,64,1,8,128]{4,3,1,0,2:T(8,128)(2,1)}, s32[2]{0:T(128)S(1)}, bf16[2,2048,1,128]{3,1,2,0:T(8,128)(2,1)}, s32[2]{0:T(128)S(1)},...) while((s32[]{:T(128)}, ...), condition=%wide.region_8.9_spmd, body=%wide.region_3.8_spmd.sunk | while | flops 566699072 | bytes 19887412 | solution.py:106
  80.2 0.9 bitcast_reduce_fusion.2
  82.9 1.0 fusion.71
  83.8 1.1 fusion.73
  87.3 0.9 bitcast_reduce_fusion.2
  90.0 1.0 fusion.71
  90.9 1.1 fusion.73
  93.0 1.0 copy.61
  94.0 4.3 %tile.9 = bf16[32,128,1024]{2,1,0:T(8,128)(2,1)} broadcast(bf16[128,1024]{1,0:T(8,128)(2,1)S(1)} %bitcast.165), dimensions={1,2} | broadcast | bytes 8650752 | tf_op jit(solution)/shard_map/tile | solution.py:116
  98.3 10.3 %all-to-all-start.2 = ((bf16[32,128,1024]{2,1,0:T(8,128)(2,1)}), bf16[32,128,1024]{2,1,0:T(8,128)(2,1)}, u32[]{:S(2)}, u32[]{:S(2)}) async-start(bf16[32,128,1024]{2,1,0:T(8,128)(2,1)} %tile.9), calls=%async_computation.2 | async-start | bytes 16777216 | tf_op jit(solution)/shard_map/all_to_all | solution.py:115
  109.6 194.1 %all-to-all-done.2 = bf16[32,128,1024]{2,1,0:T(8,128)(2,1)} async-done(((bf16[32,128,1024]{2,1,0:T(8,128)(2,1)}), bf16[32,128,1024]{2,1,0:T(8,128)(2,1)}, u32[]{:S(2)}, u32[]{:S(2)}) %all-to-all-start.2) | async-done | bytes 8388640 | tf_op jit(solution)/shard_map/all_to_all | solution.py:115
  303.8 20.4 %gather_fusion = bf16[3072,1024]{1,0:T(8,128)(2,1)} fusion(bf16[4096,1024]{1,0:T(8,128)(2,1)} %bitcast.32, s32[3072]{0:T(1024)S(1)} %broadcast_clamp_fusion), kind=kCustom, calls=%fused_computation | custom fusion | bytes 12595200 | tf_op jit(solution)/shard_map/jit(_take)/gather | solution.py:120
  324.2 7.6 %fusion.34 = bf16[3072,512]{1,0:T(8,128)(2,1)} fusion(bf16[1024,512]{1,0:T(8,128)(2,1)S(1)} %copy-done, bf16[3072,1024]{1,0:T(8,128)(2,1)} %gather_fusion, pred[3072]{0:T(1024)(128)(4,1)S(1)} %compare_and_fusion.1, pred[3072]{0:T(1024)(128)(4,1)S(1)} %fusion.50), kind=kOutput, calls=%fused_computation.49 | convolution fusion | flops 3229089792 | bytes 10491904 | tf_op jit(solution)/shard_map/dot_general | solution.py:123
  331.8 68.4 %reduce-scatter.2.cloned.1.call-done = bf16[192,512]{1,0:T(8,128)(2,1)} async-done(((bf16[3072,512]{1,0:T(8,128)(2,1)}), bf16[192,512]{1,0:T(8,128)(2,1)}) %reduce-scatter.2.cloned.1.call-update) | async-done | bytes 196624 | tf_op jit(solution)/shard_map/reduce_scatter | solution.py:122
  (54 shorter events, 9.5 us)
Async XLA Ops:
  6.5 317.6 %copy-start = (bf16[1024,512]{1,0:T(8,128)(2,1)S(1)}, bf16[1024,512]{1,0:T(8,128)(2,1)}, u32[]{:S(2)}) copy-start(bf16[1024,512]{1,0:T(8,128)(2,1)} %param.17) | copy-start | bytes 3145732
  6.5 13.0 %copy-start.2 = (bf16[2,128,1024]{2,1,0:T(8,128)(2,1)S(1)}, bf16[2,128,1024]{2,1,0:T(8,128)(2,1)}, u32[]{:S(2)}) copy-start(bf16[2,128,1024]{2,1,0:T(8,128)(2,1)} %param.15) | copy-start | bytes 1572868
  7.8 45.4 %copy-start.6 = (s32[64]{0:T(128)S(1)}, s32[64]{0:T(128)}, u32[]{:S(2)}) copy-start(s32[64]{0:T(128)} %param.19) | copy-start | bytes 772
  9.1 36.9 %all-to-all-start = ((bf16[2,128,16,128]{3,1,0,2:T(8,128)(2,1)}), bf16[2,128,16,128]{3,1,0,2:T(8,128)(2,1)S(1)}, u32[]{:S(2)}, u32[]{:S(2)}) async-start(bf16[2,128,16,128]{3,1,0,2:T(8,128)(2,1)} %bitcast.20), calls=%async_computation | async-start | bytes 2097152 | tf_op jit(solution)/shard_map/all_to_all | solution.py:95
  19.6 59.2 %copy-start.5 = (s32[2]{0:T(128)S(1)}, s32[2]{0:T(128)}, u32[]{:S(2)}) copy-start(s32[2]{0:T(128)} %param.18) | copy-start | bytes 28
  47.3 31.4 %all-to-all-start.1 = ((bf16[2,128,16,128]{3,1,0,2:T(8,128)(2,1)}), bf16[2,128,16,128]{3,1,0,2:T(8,128)(2,1)S(1)}, u32[]{:S(2)}, u32[]{:S(2)}) async-start(bf16[2,128,16,128]{3,1,0,2:T(8,128)(2,1)} %bitcast.163), calls=%async_computation.1 | async-start | bytes 2097152 | tf_op jit(solution)/shard_map/all_to_all | solution.py:94
  80.2 3.6 copy-start.1
  87.3 3.6 copy-start.1
  98.3 10.4 %copy-start.3 = (s32[64]{0:T(128)S(1)}, s32[64]{0:T(128)}, u32[]{:S(2)}) copy-start(s32[64]{0:T(128)} %param.21) | copy-start | bytes 772
  98.3 10.5 %copy-start.4 = (s32[64]{0:T(128)S(1)}, s32[64]{0:T(128)}, u32[]{:S(2)}) copy-start(s32[64]{0:T(128)} %param.20) | copy-start | bytes 772
  98.3 205.5 %all-to-all-start.2 = ((bf16[32,128,1024]{2,1,0:T(8,128)(2,1)}), bf16[32,128,1024]{2,1,0:T(8,128)(2,1)}, u32[]{:S(2)}, u32[]{:S(2)}) async-start(bf16[32,128,1024]{2,1,0:T(8,128)(2,1)} %tile.9), calls=%async_computation.2 | async-start | bytes 16777216 | tf_op jit(solution)/shard_map/all_to_all | solution.py:115
  108.7 291.6 %reduce-scatter.2.cloned.1.call-start = ((), (), s32[]{:S(2)}) async-start(), calls=%async_computation.4 | async-start | bytes 3342336 | tf_op jit(solution)/shard_map/reduce_scatter | solution.py:122
Sparse Core Ops, SparseCore 0:
  332.0 68.2 reduce-scatter.1
